TPU v7x, 32 devices: a whole 2x2x4 slice. The times are simulated.
32 devices in a mesh: gx: 4 (over x, core), gy: 2 (over y), gz: 4 (over z).
Axes of the slice: x: 2, y: 2, z: 4, core: 2. Of those that a mesh axis runs over, the one named last changes fastest.
Arguments:
- atom_embedding: bfloat16 [4, 2, 4, 64, 512], P('gx', 'gy', 'gz'), may hold values from -6 to 6
- output_adjoint: bfloat16 [4, 2, 4, 64, 512], P('gx', 'gy', 'gz'), may hold values from -6 to 6
- fractional_coords: float32 [4, 2, 4, 3, 512], P('gx', 'gy', 'gz'), may hold values from 0 to 1, as said below
- element_labels: int32 [4, 2, 4, 512], P('gx', 'gy', 'gz'), may hold values from 0 to 3
- adjacent_ghost_entries: int32 [4, 2, 4, 16, 512], P('gx', 'gy', 'gz'), may hold values from 0 to 13823, as said below
- miller_triples: int32 [3, 2048], replicated, may hold values from -8 to 8
- reciprocal_kernel: float32 [2048, 64], replicated, may hold values from 0.02 to 0.2
- channel_mixing_matrix: bfloat16 [64, 64], replicated, may hold values from -0.75 to 0.75
- element_channel_factor: float32 [4, 64], replicated, may hold values from 0.25 to 1.75
- distance_kernel: float32 [16, 64], replicated, may hold values from -1.5 to 1.5
Outputs:
- atom_grad: bfloat16 [4, 2, 4, 64, 512], P('gx', 'gy', 'gz')
- position_grad: float32 [4, 2, 4, 3, 512], P('gx', 'gy', 'gz')
- weight_grad: float32 [64, 64], replicated
- radial_grad: float32 [16, 64], replicated
- filter_grad: float32 [2048, 64], P(('gx', 'gy', 'gz'))
Inputs may be any that keep to these rules, and one draw needn't show every extreme that they name: `adjacent_ghost_entries`: the atoms of a brick form 32 blocks of 16 in order; block q < 27 is the cell of offset (q // 9 - 1, (q // 3) % 3 - 1, q % 3 - 1) of the brick, blocks 27 to 31 lie in its central cell. A ghost entry e names atom e % 512 of slot e // 512; an entry in a slot of offset o names an atom of a block whose cell offset equals -o in every dimension where o is not zero, and o is zero in every dimension where the listing atom's cell offset is zero; every slot occurs. `fractional_coords`: an atom of a block whose cell offset is -1 or 1 in a dimension lies within a quarter of the brick length of that face in that dimension. `miller_triples`: integer components; any triple may occur, the zero triple too.
All inputs are finite; a program needn't handle non-finite values.
Results may differ from a plain program's by a relative error of at most 0.0053.
Values may be sent and summed in bfloat16 or wider, within the bound.
A program may use at most 128 MiB of HBM per device.

v0:
```python
import functools
import itertools
import math

import jax
import jax.numpy as jnp
from jax import lax
from jax.experimental import pallas as pl
from jax.experimental.pallas import tpu as pltpu
from jax.sharding import PartitionSpec as P

AXES = ("gx", "gy", "gz")
reach_sq = 0.75
LANES = 128
VMEM_LIMIT = 60 * 1024 * 1024
f32 = jnp.float32
bf16 = jnp.bfloat16
NT = (((1,), (1,)), ((), ()))
OFFSETS = list(itertools.product((-1, 0, 1), repeat=3))
POS_HI, POS_MID, POS_LO, POS_OFF, LABEL = 64, 72, 80, 88, 96
GATHERED = 96


def dot(a, b):
    return jnp.dot(a, b, preferred_element_type=f32)


def dot_nt(a, b):
    return lax.dot_general(a, b, NT, preferred_element_type=f32)


def split2(x):
    hi = x.astype(bf16)
    return hi, (x - hi.astype(f32)).astype(bf16)


def sincos_turns(u):
    q = jnp.round(u * 2.0)
    x = (u - 0.5 * q) * (2.0 * math.pi)
    odd = q - 2.0 * jnp.floor(q * 0.5)
    sign = 1.0 - 2.0 * odd
    y = x * x
    s = -1.0 / 39916800.0
    for c in (1.0 / 362880.0, -1.0 / 5040.0, 1.0 / 120.0, -1.0 / 6.0, 1.0):
        s = s * y + c
    c_ = 1.0 / 479001600.0
    for c in (-1.0 / 3628800.0, 1.0 / 40320.0, -1.0 / 720.0, 1.0 / 24.0, -0.5, 1.0):
        c_ = c_ * y + c
    return c_ * sign, s * x * sign


def phase_kernel(h_ref, dy_ref, pos_ref, turns_ref, label_ref, mil_ref,
                 cos_ref, sin_ref, part_ref, table_ref):
    channels, atoms = h_ref.shape
    rows = mil_ref.shape[0]
    step = 128
    h = h_ref[...]
    stacked = jnp.concatenate([h, dy_ref[...]], axis=0)
    pos = pos_ref[...]
    hi = pos.astype(bf16).astype(f32)
    mid = (pos - hi).astype(bf16).astype(f32)
    lo = pos - hi - mid
    blank = jnp.zeros((LANES - LABEL - 8, atoms), f32)
    feats = jnp.concatenate(
        [h.astype(f32), hi, mid, lo, jnp.zeros((8, atoms), f32), label_ref[...], blank], axis=0)
    table_ref[...] = jnp.transpose(feats).astype(bf16).reshape(table_ref.shape)
    w0, w1, w2 = turns_ref[0:1, :], turns_ref[1:2, :], turns_ref[2:3, :]

    def body(i, _):
        at = pl.ds(pl.multiple_of(i * step, step), step)
        m = mil_ref[at, :]
        u = m[:, 0:1] * w0 + m[:, 1:2] * w1 + m[:, 2:3] * w2
        c, s = sincos_turns(u)
        c = c.astype(bf16)
        s = s.astype(bf16)
        cos_ref[at, :] = c
        sin_ref[at, :] = s
        part_ref[at, 0:2 * channels] = dot_nt(c, stacked).astype(bf16)
        part_ref[at, 2 * channels:4 * channels] = dot_nt(s, stacked).astype(bf16)
        return 0

    lax.fori_loop(0, rows // step, body, 0)


def coords(linear, sizes):
    nx, ny, nz = sizes
    return (linear // (ny * nz), (linear // nz) % ny, linear % nz)


def my_linear(sizes):
    nx, ny, nz = sizes
    return (lax.axis_index("gx") * ny + lax.axis_index("gy")) * nz + lax.axis_index("gz")


def neighbour(offset, sizes, flip):
    return tuple(
        lax.rem(lax.axis_index(a) + (n - flip * o), n) if flip > 0
        else lax.rem(lax.axis_index(a) + (n + o), n)
        for a, o, n in zip(AXES, offset, sizes))


def enter(n, sizes):
    me = my_linear(sizes)
    barrier = pltpu.get_barrier_semaphore()

    def signal(i, _):
        pl.semaphore_signal(barrier, inc=1, device_id=coords(lax.rem(me + i, n), sizes),
                            device_id_type=pl.DeviceIdType.MESH)
        return 0

    lax.fori_loop(1, n, signal, 0)
    pl.semaphore_wait(barrier, n - 1)
    return me


def span(o, low, high):
    return pl.ds(1, 3) if o == 0 else pl.ds(high if o > 0 else low, 1)


def own_span(o):
    return pl.ds(0, 3) if o == 0 else pl.ds(0 if o > 0 else 2, 1)


def local_span(o):
    return pl.ds(0, 3 if o == 0 else 1)


def all_bytes(ref, n, sem):
    part = ref.at[pl.ds(0, n - 1)]
    return pltpu.make_async_copy(part, part, sem)


def gather_kernel(sizes, norm_atoms, norm_k, table_ref, part_ref, kf_ref,
                  ext_ref, coef_ref, fg_ref, halo, recv, hs, hr, ss, rs):
    n = sizes[0] * sizes[1] * sizes[2]
    me = enter(n, sizes)
    copies = []
    for o in OFFSETS:
        if o == (0, 0, 0):
            continue
        src = table_ref.at[tuple(own_span(d) for d in o)]
        dst = halo.at[tuple(span(d, 0, 4) for d in o)]
        slot = 9 * (o[0] + 1) + 3 * (o[1] + 1) + o[2] + 1
        copy = pltpu.make_async_remote_copy(
            src_ref=src, dst_ref=dst, send_sem=hs.at[slot], recv_sem=hr.at[slot],
            device_id=neighbour(o, sizes, 1), device_id_type=pl.DeviceIdType.MESH)
        copy.start()
        copies.append(copy)

    def send(i, _):
        to = lax.rem(me + i, n)
        pltpu.make_async_remote_copy(
            src_ref=part_ref.at[to], dst_ref=recv.at[i - 1], send_sem=ss, recv_sem=rs,
            device_id=coords(to, sizes), device_id_type=pl.DeviceIdType.MESH).start()
        return 0

    lax.fori_loop(1, n, send, 0)
    for copy in copies:
        copy.wait()
    ext_ref[...] = halo[...]
    ext_ref[1:4, 1:4, 1:4] = table_ref[...]
    all_bytes(part_ref, n, ss).wait()
    all_bytes(recv, n, rs).wait()

    def add(i, total):
        return total + recv[i].astype(f32)

    total = lax.fori_loop(0, n - 1, add, part_ref[me].astype(f32))
    ch = kf_ref.shape[1]
    kf = kf_ref[...]
    cs = total[:, 0:ch] * norm_atoms
    cb = total[:, ch:2 * ch] * norm_k
    sst = total[:, 2 * ch:3 * ch] * norm_atoms
    sb = total[:, 3 * ch:4 * ch] * norm_k
    coef_ref[...] = jnp.concatenate(
        [norm_atoms * kf * cb, norm_k * kf * cs, norm_atoms * kf * sb, norm_k * kf * sst],
        axis=1).astype(bf16)
    fg_ref[...] = cs * cb + sst * sb


def short_kernel(basis_count, ext_ref, extra_ref, cid_ref, pos_ref, dy_ref, mix_ref, gain_ref,
                 shift_ref, dk_ref, dkt_ref, grad_ref, own_ref, wr_ref,
                 oh, near, filt, vals, ht, zg, acc, agg, gout, psum, rad):
    ep = oh.shape[1]
    nbr, atoms = cid_ref.shape
    channels = dy_ref.shape[0]
    cells = 125 * 16
    extras = extra_ref.shape[0] * 16
    pad = ep - cells - extras
    table = jnp.concatenate(
        [ext_ref[...].reshape(cells, LANES), extra_ref[...].reshape(extras, LANES),
         jnp.zeros((pad, LANES), bf16)], axis=0)
    tf = table.astype(f32)
    label = tf[:, LABEL:LABEL + 1]
    gains = jnp.zeros((ep, LANES), f32)
    for s in range(gain_ref.shape[0]):
        gains = jnp.where(label == float(s), gain_ref[s:s + 1, :], gains)
    zg[...] = gains
    z = dot(table, mix_ref[...]) * gains
    lane = lax.broadcasted_iota(jnp.int32, (ep, LANES), 1)
    full = jnp.where(lane < channels, z, tf) + shift_ref[...]
    vals[...] = jnp.transpose(full).astype(bf16)
    ht[...] = jnp.transpose(tf).astype(bf16)
    spacing = reach_sq / (basis_count - 1)
    centre = lax.broadcasted_iota(jnp.int32, (basis_count, 1), 0).astype(f32) * spacing
    inv = 1.0 / (2.0 * spacing)
    own = pos_ref[...]
    agg[...] = jnp.zeros_like(agg)
    psum[...] = jnp.zeros_like(psum)
    acc[...] = jnp.zeros_like(acc)
    rad[...] = jnp.zeros_like(rad)
    one, nil = jnp.ones((), bf16), jnp.zeros((), bf16)
    dkt_hi, dkt_lo = split2(dkt_ref[...])
    dkt3 = jnp.concatenate([dkt_hi, dkt_lo, dkt_hi], axis=1)
    dk_hi, dk_lo = split2(dk_ref[...])
    dk3 = jnp.concatenate([dk_hi, dk_lo, dk_hi], axis=1)
    tile = 256

    def geometry(j):
        at = near[j]
        place = at[POS_HI:POS_HI + 8] + at[POS_MID:POS_MID + 8] + at[POS_LO:POS_LO + 8]
        rel = (place + at[POS_OFF:POS_OFF + 8]) - own
        d2 = jnp.sum(rel * rel, axis=0, keepdims=True)
        arg = (d2 - centre) * inv
        return at, rel, arg, jnp.exp(-(arg * arg))

    def forward(j, _):
        cid = cid_ref[pl.ds(j, 1), :]
        high = cid // tile
        low = cid - high * tile
        for start in range(0, ep, tile):
            size = min(tile, ep - start)
            want = jnp.where(high == start // tile, low, -1).astype(f32).astype(bf16)
            rows = lax.broadcasted_iota(jnp.int32, (size, atoms), 0).astype(f32).astype(bf16)
            oh[j, start:start + size, :] = jnp.where(rows == want, one, nil)
        near[j] = dot(vals[0:GATHERED, :], oh[j])
        at, rel, arg, basis = geometry(j)
        b_hi, b_lo = split2(basis)
        f = dot(dkt3, jnp.concatenate([b_hi, b_hi, b_lo], axis=0))
        filt[j] = f
        agg[...] += f * at[0:channels]
        return 0

    lax.fori_loop(0, nbr, forward, 0)
    scale = nbr ** (-0.5)
    v = agg[...] * scale
    sg = 1.0 / (1.0 + jnp.exp(-v))
    gout[...] = dy_ref[...].astype(f32) * (sg * (1.0 + v * (1.0 - sg))) * scale

    def backward(j, _):
        g = gout[...]
        at, rel, arg, basis = geometry(j)
        dz = (filt[j] * g).astype(bf16)
        df_hi, df_lo = split2(at[0:channels] * g)
        db = dot(dk3, jnp.concatenate([df_hi, df_hi, df_lo], axis=0))
        dd2 = jnp.sum(db * basis * arg, axis=0, keepdims=True) * (-2.0 * inv)
        drel = 2.0 * rel * dd2
        psum[...] += drel
        d_hi = drel.astype(bf16).astype(f32)
        dvals = jnp.concatenate(
            [dz, jnp.concatenate([d_hi, drel - d_hi], axis=0).astype(bf16)], axis=0)
        acc[...] += dot_nt(oh[j], dvals)
        b_hi, b_lo = split2(basis)
        rad[...] += dot_nt(jnp.concatenate([b_hi, b_lo, b_hi], axis=1),
                           jnp.concatenate([df_hi, df_hi, df_lo], axis=1))
        return 0

    lax.fori_loop(0, nbr, backward, 0)
    g = acc[...]
    zgrad = g[:, 0:channels]
    pg = g[:, channels:channels + 8] + g[:, channels + 8:channels + 16]
    p_hi = pg.astype(bf16).astype(f32)
    grad_ref[...] = jnp.concatenate(
        [zgrad, p_hi, pg - p_hi, jnp.zeros((ep, LANES - channels - 16), f32)],
        axis=1).astype(bf16).reshape(grad_ref.shape)
    own_ref[...] = psum[...]
    scaled = (zgrad * zg[:, 0:channels]).astype(bf16)
    w = dot(ht[0:channels, :], scaled)
    half = channels // 2
    r = rad[...]
    hb = basis_count // 2
    wr_ref[...] = jnp.concatenate(
        [jnp.concatenate([w[:half], w[half:]], axis=1),
         jnp.concatenate([r[:hb], r[hb:]], axis=1),
         jnp.zeros((wr_ref.shape[0] - half - hb, LANES), f32)], axis=0).astype(bf16)


def return_kernel(sizes, channels, basis_count, grad_ref, coef_ref, wr_ref,
                  home_ref, extra_ref, coefs_ref, weight_ref, radial_ref,
                  back, crecv, wrecv, hs, hr, cs, cr, ws, wrs):
    n = sizes[0] * sizes[1] * sizes[2]
    me = enter(n, sizes)
    copies = []
    for o in OFFSETS:
        if o == (0, 0, 0):
            continue
        slot = 9 * (o[0] + 1) + 3 * (o[1] + 1) + o[2] + 1
        copy = pltpu.make_async_remote_copy(
            src_ref=grad_ref.at[tuple(span(d, 0, 4) for d in o)],
            dst_ref=back.at[(slot,) + tuple(local_span(d) for d in o)],
            send_sem=hs.at[slot], recv_sem=hr.at[slot],
            device_id=neighbour(o, sizes, -1), device_id_type=pl.DeviceIdType.MESH)
        copy.start()
        copies.append((o, slot, copy))

    def send(i, _):
        to = coords(lax.rem(me + i, n), sizes)
        pltpu.make_async_remote_copy(
            src_ref=coef_ref.at[0], dst_ref=crecv.at[i - 1], send_sem=cs, recv_sem=cr,
            device_id=to, device_id_type=pl.DeviceIdType.MESH).start()
        pltpu.make_async_remote_copy(
            src_ref=wr_ref.at[0], dst_ref=wrecv.at[i - 1], send_sem=ws, recv_sem=wrs,
            device_id=to, device_id_type=pl.DeviceIdType.MESH).start()
        return 0

    lax.fori_loop(1, n, send, 0)
    home_ref[...] = grad_ref[1:4, 1:4, 1:4].astype(f32)
    for o, slot, copy in copies:
        copy.wait()
        at = tuple(slice(0, 3) if d == 0 else (slice(0, 1) if d > 0 else slice(2, 3)) for d in o)
        loc = (slot,) + tuple(slice(0, 3 if d == 0 else 1) for d in o)
        home_ref[at] += back[loc].astype(f32)
    all_bytes(wrecv, n, ws).wait()
    all_bytes(wrecv, n, wrs).wait()
    all_bytes(crecv, n, cs).wait()
    all_bytes(crecv, n, cr).wait()
    wrecv[n - 1] = wr_ref[0]

    def add(i, total):
        return total + wrecv[lax.rem(me - i + n + n - 1, n)].astype(f32)

    total = lax.fori_loop(0, n, add, jnp.zeros(wr_ref.shape[1:], f32))
    half, hb = channels // 2, basis_count // 2
    weight_ref[0:half] = total[0:half, 0:channels]
    weight_ref[half:channels] = total[0:half, channels:2 * channels]
    radial_ref[0:hb] = total[half:half + hb, 0:channels]
    radial_ref[hb:basis_count] = total[half:half + hb, channels:2 * channels]
    coefs_ref[me] = coef_ref[0]

    def place(i, _):
        coefs_ref[lax.rem(me - i + n, n)] = crecv[i - 1]
        return 0

    lax.fori_loop(1, n, place, 0)


def final_kernel(coef_ref, cos_ref, sin_ref, h_ref, dy_ref, milt_ref, turn_ref, home_ref,
                 extra_ref, own_ref, gain_ref, mix_ref, atom_ref, pos_ref, eh, ep_):
    rows = coef_ref.shape[0]
    channels, atoms = h_ref.shape
    step = 256
    stacked = jnp.concatenate([h_ref[...], dy_ref[...]], axis=0)
    eh[...] = jnp.zeros_like(eh)
    ep_[...] = jnp.zeros_like(ep_)

    def body(i, _):
        at = pl.ds(pl.multiple_of(i * step, step), step)
        piece = coef_ref[at, :]
        c, s = cos_ref[at, :], sin_ref[at, :]
        turned = jnp.transpose(piece.astype(f32)).astype(bf16)
        eh[...] += dot(turned[0:channels], c) + dot(turned[2 * channels:3 * channels], s)
        u = dot(piece[:, 0:2 * channels], stacked)
        v = dot(piece[:, 2 * channels:4 * channels], stacked)
        hi, lo = split2(v * c.astype(f32) - u * s.astype(f32))
        m = milt_ref[i]
        ep_[...] += dot(m, hi) + dot(m, lo)
        return 0

    lax.fori_loop(0, rows // step, body, 0)
    blocks = 27 * 16
    home = jnp.concatenate(
        [home_ref[...].reshape(blocks, LANES),
         extra_ref[...].astype(f32).reshape(atoms - blocks, LANES)], axis=0)
    g = jnp.transpose(home)
    zscaled = (g[0:channels] * gain_ref[...]).astype(bf16)
    short = dot(mix_ref[...], zscaled)
    atom_ref[...] = (dy_ref[...].astype(f32) + eh[...] + short).astype(bf16)
    pos_short = g[channels:channels + 8] + g[channels + 8:channels + 16] - own_ref[...]
    pos_ref[...] = ep_[0:8] * turn_ref[...] + pos_short


def vmem(count):
    return [pl.BlockSpec(memory_space=pltpu.VMEM)] * count


def params(**more):
    return pltpu.CompilerParams(vmem_limit_bytes=VMEM_LIMIT, **more)


def shards(sizes, atom_embedding, output_adjoint, fractional_coords, element_labels,
           adjacent_ghost_entries, miller_triples, reciprocal_kernel, channel_mixing_matrix,
           element_channel_factor, distance_kernel):
    n = sizes[0] * sizes[1] * sizes[2]
    shape = jax.ShapeDtypeStruct
    h = atom_embedding[0, 0, 0]
    dy = output_adjoint[0, 0, 0]
    pos = fractional_coords[0, 0, 0]
    channels, atoms = h.shape
    rows = miller_triples.shape[1]
    share = rows // n
    basis_count = distance_kernel.shape[0]
    norm_atoms = (atoms * n) ** (-0.5)
    norm_k = rows ** (-0.5)
    counts = jnp.array(sizes, f32)
    anchor = jnp.stack([lax.axis_index(a) for a in AXES]).astype(f32)
    pos8 = jnp.pad(pos, ((0, 5), (0, 0)))
    turns8 = jnp.pad((pos + anchor[:, None]) / counts[:, None], ((0, 5), (0, 0)))
    labels = element_labels[0, 0, 0]
    label8 = jnp.pad(labels.astype(f32)[None, :], ((0, 7), (0, 0)))
    miller = miller_triples.astype(f32)
    mil8 = jnp.pad(miller.T, ((0, 0), (0, 5)))
    cos_all, sin_all, part, table = pl.pallas_call(
        phase_kernel,
        out_shape=(shape((rows, atoms), bf16), shape((rows, atoms), bf16),
                   shape((rows, 4 * channels), bf16), shape((atoms // 16, 16, LANES), bf16)),
        in_specs=vmem(6), out_specs=tuple(vmem(4)), compiler_params=params(), name="phases",
    )(h, dy, pos8, turns8, label8, mil8)

    me = lax.axis_index(AXES)
    kf = lax.dynamic_slice_in_dim(reciprocal_kernel, me * share, share, 0)
    dma = pltpu.SemaphoreType.DMA
    ext, coef, filter_share = pl.pallas_call(
        functools.partial(gather_kernel, sizes, norm_atoms, norm_k),
        out_shape=(shape((5, 5, 5, 16, LANES), bf16), shape((share, 4 * channels), bf16),
                   shape((share, channels), f32)),
        in_specs=vmem(3), out_specs=tuple(vmem(3)),
        scratch_shapes=[pltpu.VMEM((5, 5, 5, 16, LANES), bf16),
                        pltpu.VMEM((n, share, 4 * channels), bf16),
                        dma((27,)), dma((27,)), dma, dma],
        compiler_params=params(collective_id=0, has_side_effects=True), name="halo",
    )(table[:27].reshape(3, 3, 3, 16, LANES), part.reshape(n, share, 4 * channels), kf)

    e = adjacent_ghost_entries[0, 0, 0]
    slot, atom = e // atoms, e % atoms
    block = atom // 16
    cell = [slot // 9 - 1, (slot // 3) % 3 - 1, slot % 3 - 1]
    sub = [block // 9 - 1, (block // 3) % 3 - 1, block % 3 - 1]
    x, y, z = [t + 3 * o + 2 for t, o in zip(sub, cell)]
    place = jnp.where(block < 27, 25 * x + 5 * y + z, 125 + block - 27)
    cid = place * 16 + atom % 16
    nbr = e.shape[0]
    total = (125 + atoms // 16 - 27) * 16
    ep = -(-total // LANES) * LANES
    import numpy as np
    shift = np.zeros((ep, LANES), np.float32)
    for i, (cx, cy, cz) in enumerate(itertools.product(range(5), repeat=3)):
        for d, q in enumerate((cx, cy, cz)):
            shift[16 * i:16 * i + 16, POS_OFF + d] = -1.0 if q == 0 else (1.0 if q == 4 else 0.0)
    mixp = jnp.pad(channel_mixing_matrix, ((0, LANES - channels), (0, LANES - channels)))
    gainp = jnp.pad(element_channel_factor, ((0, 0), (0, LANES - channels)))
    wr_rows = -(-(channels // 2 + basis_count // 2) // 16) * 16
    grad, own, wr = pl.pallas_call(
        functools.partial(short_kernel, basis_count),
        out_shape=(shape((ep // 16, 16, LANES), bf16), shape((8, atoms), f32),
                   shape((wr_rows, LANES), bf16)),
        in_specs=vmem(10), out_specs=tuple(vmem(3)),
        scratch_shapes=[pltpu.VMEM((nbr, ep, atoms), bf16),
                        pltpu.VMEM((nbr, GATHERED, atoms), f32),
                        pltpu.VMEM((nbr, channels, atoms), f32),
                        pltpu.VMEM((LANES, ep), bf16), pltpu.VMEM((LANES, ep), bf16),
                        pltpu.VMEM((ep, LANES), f32),
                        pltpu.VMEM((ep, channels + 16), f32),
                        pltpu.VMEM((channels, atoms), f32), pltpu.VMEM((channels, atoms), f32),
                        pltpu.VMEM((8, atoms), f32), pltpu.VMEM((basis_count, channels), f32)],
        compiler_params=params(), name="short",
    )(ext, table[27:], cid, pos8, dy, mixp, gainp, jnp.asarray(shift), distance_kernel,
      distance_kernel.T)

    extras = atoms // 16 - 27
    home, coefs, weight_grad, radial_grad = pl.pallas_call(
        lambda g, c, w, a, b, r, s, *rest: return_kernel(
            sizes, channels, basis_count, g, c, w, a, None, b, r, s, *rest),
        out_shape=(shape((3, 3, 3, 16, LANES), f32), shape((n, share, 4 * channels), bf16),
                   shape((channels, channels), f32), shape((basis_count, channels), f32)),
        in_specs=vmem(3), out_specs=tuple(vmem(4)),
        scratch_shapes=[pltpu.VMEM((27, 3, 3, 3, 16, LANES), bf16),
                        pltpu.VMEM((n - 1, share, 4 * channels), bf16),
                        pltpu.VMEM((n, wr_rows, LANES), bf16),
                        dma((27,)), dma((27,)), dma, dma, dma, dma],
        compiler_params=params(collective_id=1, has_side_effects=True), name="home",
    )(grad[:125].reshape(5, 5, 5, 16, LANES), coef[None], wr[None])

    onehot = (labels[None, :] == jnp.arange(element_channel_factor.shape[0])[:, None])
    gains = lax.dot_general(element_channel_factor, onehot.astype(f32), (((0,), (0,)), ((), ())),
                            precision=lax.Precision.HIGHEST)
    milt = jnp.pad(miller.astype(bf16), ((0, 13), (0, 0)))
    milt = jnp.transpose(milt.reshape(16, rows // 256, 256), (1, 0, 2))
    turn = jnp.pad((2.0 * math.pi) / counts, (0, 5))[:, None] * jnp.ones((1, atoms), f32)
    atom_grad, pos_grad = pl.pallas_call(
        final_kernel,
        out_shape=(shape((channels, atoms), bf16), shape((8, atoms), f32)),
        in_specs=vmem(12), out_specs=tuple(vmem(2)),
        scratch_shapes=[pltpu.VMEM((channels, atoms), f32), pltpu.VMEM((16, atoms), f32)],
        compiler_params=params(), name="final",
    )(coefs.reshape(rows, 4 * channels), cos_all, sin_all, h, dy, milt, turn, home,
      grad[125:125 + extras], own, gains, channel_mixing_matrix)
    return (atom_grad[None, None, None], pos_grad[None, None, None, 0:3], weight_grad,
            radial_grad, filter_share)


def solution(mesh):
    sizes = tuple(mesh.shape[a] for a in AXES)
    brick = P("gx", "gy", "gz", None, None)
    return jax.shard_map(
        functools.partial(shards, sizes),
        mesh=mesh,
        in_specs=(brick, brick, brick, P("gx", "gy", "gz", None), brick,
                  P(), P(), P(), P(), P()),
        out_specs=(brick, brick, P(), P(), P(("gx", "gy", "gz"), None)),
        check_vma=False,
    )
```

profile of v0, /device:TPU:0, one launch (start us, length us, event | category | flops | bytes accessed | tf_op | source)
XLA Modules:
  0.0 154.9 jit_solution(15020866174283489511)
XLA Ops:
  0.7 1.0 copy-done
  1.7 0.1 constant_dynamic-slice_fusion
  1.8 0.7 copy.33.kf_ref
  2.5 0.1 add_convert_fusion
  2.5 0.8 add_multiply_fusion
  3.3 0.6 pad.32.turns_ref
  3.9 0.8 convert_convert_fusion
  4.7 0.4 copy.27
  5.1 1.1 pad.34.mil_ref
  6.2 0.6 pad.31.pos_ref
  6.8 0.6 pad.33.label_ref
  7.4 12.9 %phases.1 = (bf16[2048,512]{1,0:T(8,128)(2,1)}, bf16[2048,512]{1,0:T(8,128)(2,1)}, bf16[2048,256]{1,0:T(8,128)(2,1)}, bf16[32,16,128]{2,1,0:T(8,128)(2,1)}) custom-call(bf16[64,512]{1,0:T(8,128)(2,1)} %bitcast.60, bf16[64,512]{1,0:T(8,128)(2,1)} %bitcast.56, f32[8,512]{1,0:T(8,128)} %pad.31.pos_ref, f32[8,512]{1,0:T(8,128)} %pad.32.turns_ref, ...), custom_call_target="tpu_custom_call" | custom-call | tf_op jit(solution)/shard_map/phases/pallas_call | solution.py:412
  20.3 1.6 %slice.15 = bf16[27,16,128]{2,1,0:T(8,128)(2,1)} slice(bf16[32,16,128]{2,1,0:T(8,128)(2,1)} %get-tuple-element.21), slice={[0:27], [0:16], [0:128]} | slice | bytes 221184 | tf_op jit(solution)/shard_map/slice | solution.py:431
  21.9 37.9 %halo.1 = (bf16[5,5,5,16,128]{4,3,2,1,0:T(8,128)(2,1)}, bf16[64,256]{1,0:T(8,128)(2,1)}, f32[64,64]{1,0:T(8,128)}) custom-call(bf16[3,3,3,16,128]{4,3,2,1,0:T(8,128)(2,1)} %bitcast.59, bf16[32,64,256]{2,1,0:T(8,128)(2,1)} %bitcast.55, f32[64,64]{1,0:T(8,128)} %copy.33.kf_ref), custom_call_target="tpu_custom_call" | custom-call | tf_op jit(solution)/shard_map/halo/pallas_call | solution.py:422
  59.8 1.3 slice.16.extra_ref
  61.1 0.7 copy.29
  61.8 0.8 fusion.8.cid_ref
  62.7 0.6 pad.35.mix_ref
  63.3 0.6 pad.36.gain_ref
  63.9 30.1 %short.1 = (bf16[136,16,128]{2,1,0:T(8,128)(2,1)}, f32[8,512]{1,0:T(8,128)}, bf16[48,128]{1,0:T(8,128)(2,1)}) custom-call(bf16[5,5,5,16,128]{4,3,2,1,0:T(8,128)(2,1)} %get-tuple-element.23.ext_ref, bf16[5,16,128]{2,1,0:T(8,128)(2,1)} %slice.16.extra_ref, s32[16,512]{1,0:T(8,128)} %fusion.8.cid_ref, f32[8,512]{1,0:T(8,128)} %pad.31.pos_ref, ...), custom_call_target="tpu_custom_call" | custom-call | tf_op jit(solution)/shard_map/short/pallas_call | solution.py:452
  94.0 1.9 %slice.17 = bf16[125,16,128]{2,1,0:T(8,128)(2,1)} slice(bf16[136,16,128]{2,1,0:T(8,128)(2,1)} %get-tuple-element.24), slice={[0:125], [0:16], [0:128]} | slice | bytes 1024000 | tf_op jit(solution)/shard_map/slice | solution.py:481
  95.8 43.6 %home.1 = (f32[3,3,3,16,128]{4,3,2,1,0:T(8,128)}, bf16[32,64,256]{2,1,0:T(8,128)(2,1)}, f32[64,64]{1,0:T(8,128)}, f32[16,64]{1,0:T(8,128)}) custom-call(bf16[5,5,5,16,128]{4,3,2,1,0:T(8,128)(2,1)} %bitcast.53, bf16[1,64,256]{2,1,0:T(8,128)(2,1)} %bitcast.65, bf16[1,48,128]{2,1,0:T(8,128)(2,1)} %bitcast.67), custom_call_target="tpu_custom_call" | custom-call | tf_op jit(solution)/shard_map/home/pallas_call | solution.py:470
  139.5 1.3 slice.18.extra_ref
  140.8 0.6 copy.39
  141.5 0.9 convolution_bitcast_fusion.gain_ref
  142.4 0.7 mul.50.turn_ref
  143.1 8.6 %final.1 = (bf16[64,512]{1,0:T(8,128)(2,1)}, f32[8,512]{1,0:T(8,128)}) custom-call(bf16[2048,256]{1,0:T(8,128)(2,1)} %bitcast.54, bf16[2048,512]{1,0:T(8,128)(2,1)} %get-tuple-element.28.cos_ref, bf16[2048,512]{1,0:T(8,128)(2,1)} %get-tuple-element.29.sin_ref, bf16[64,512]{1,0:T(8,128)(2,1)} %bitcast.61, bf16[64,512]{1,0:T(8,128)(2,1)} %bitcast.58, ...), custom_call_target="tpu_custom_call" | custom-call | tf_op jit(solution)/shard_map/final/pallas_call | solution.py:489
  151.7 0.7 slice_bitcast_fusion
  152.4 0.6 copy.31
  153.0 0.6 copy.44
  153.6 0.6 copy.45
  154.2 0.6 copy.46
  (24 shorter events, 0.1 us)
Async XLA Ops:
  0.6 1.0 copy-start
  0.6 5.6 %copy-start.6 = (f32[1,1,1,3,512]{4,2,3,1,0:T(1,128)S(1)}, f32[1,1,1,3,512]{4,2,3,1,0:T(1,128)}, u32[]{:S(2)}) copy-start(f32[1,1,1,3,512]{4,2,3,1,0:T(1,128)} %param.14) | copy-start | bytes 18436
  0.7 6.2 %copy-start.7 = (s32[1,1,1,512]{3,2,1,0:T(1,128)S(1)}, s32[1,1,1,512]{3,2,1,0:T(1,128)}, u32[]{:S(2)}) copy-start(s32[1,1,1,512]{3,2,1,0:T(1,128)} %param.15) | copy-start | bytes 6148
  5.1 56.1 %copy-start.2 = (f32[16,64]{1,0:T(8,128)S(1)}, f32[16,64]{1,0:T(8,128)}, u32[]{:S(2)}) copy-start(f32[16,64]{1,0:T(8,128)} %dk_ref.1) | copy-start | bytes 12292
  5.1 56.8 %copy-start.3 = (s32[1,1,1,16,512]{4,3,2,1,0:T(8,128)S(1)}, s32[1,1,1,16,512]{4,3,2,1,0:T(8,128)}, u32[]{:S(2)}) copy-start(s32[1,1,1,16,512]{4,3,2,1,0:T(8,128)} %param.16) | copy-start | bytes 98308
  5.1 57.6 %copy-start.1 = (bf16[64,64]{1,0:T(8,128)(2,1)S(1)}, bf16[64,64]{1,0:T(8,128)(2,1)}, u32[]{:S(2)}) copy-start(bf16[64,64]{1,0:T(8,128)(2,1)} %mix_ref.1) | copy-start | bytes 24580
  5.1 58.2 %copy-start.8 = (f32[4,64]{1,0:T(4,128)S(1)}, f32[4,64]{1,0:T(4,128)}, u32[]{:S(2)}) copy-start(f32[4,64]{1,0:T(4,128)} %param.20) | copy-start | bytes 3076
  59.8 82.6 %copy-start.10 = (f32[8]{0:T(128)S(1)}, f32[8]{0:T(128)}, u32[]{:S(2)}) copy-start(f32[8]{0:T(128)} %constant.157) | copy-start | bytes 100
  143.1 10.0 %copy-start.5 = (f32[64,64]{1,0:T(8,128)S(1)}, f32[64,64]{1,0:T(8,128)}, u32[]{:S(2)}) copy-start(f32[64,64]{1,0:T(8,128)} %get-tuple-element.61) | copy-start | bytes 49156
  143.1 10.6 %copy-start.9 = (f32[16,64]{1,0:T(8,128)S(1)}, f32[16,64]{1,0:T(8,128)}, u32[]{:S(2)}) copy-start(f32[16,64]{1,0:T(8,128)} %get-tuple-element.62) | copy-start | bytes 12292
  143.1 11.2 %copy-start.4 = (f32[64,64]{1,0:T(8,128)S(1)}, f32[64,64]{1,0:T(8,128)}, u32[]{:S(2)}) copy-start(f32[64,64]{1,0:T(8,128)} %get-tuple-element.63) | copy-start | bytes 49156
where the time goes:
time: 155 us
  Pallas kernels  133 us (86%)
  local copies, waits for them, and re-layouts  17.6 us (11%)
  other arithmetic  2.46 us (2%)
    pallas_call x1, Pallas kernels, shards(): pl.pallas_call(lambda g, c, w, a, b, r, s, *rest: return_kernel(sizes, ch...  43.6 us
    pallas_call x1, Pallas kernels, shards(): pl.pallas_call(functools.partial(gather_kernel, sizes, norm_atoms, norm_k...  37.9 us
    pallas_call x1, Pallas kernels, shards(): pl.pallas_call(functools.partial(short_kernel, basis_count), out_shape=(s...  30.1 us
    pallas_call x1, Pallas kernels, shards(): pl.pallas_call(phase_kernel, out_shape=(shape((rows, atoms), bf16), shape...  12.9 us
    pallas_call x1, Pallas kernels, shards(): pl.pallas_call(final_kernel, out_shape=(shape((channels, atoms), bf16), s...  8.62 us
    unnamed x29, local copies, waits for them, and re-layouts  4.89 us

commit v1 on v0

v1 whole, which is shorter than its diff:
```python
import functools
import itertools
import math

import jax
import jax.numpy as jnp
import numpy as np
from jax import lax
from jax.experimental import pallas as pl
from jax.experimental.pallas import tpu as pltpu
from jax.sharding import PartitionSpec as P

AXES = ("gx", "gy", "gz")
reach_sq = 0.75
LANES = 128
VMEM_LIMIT = 60 * 1024 * 1024
f32 = jnp.float32
bf16 = jnp.bfloat16
NT = (((1,), (1,)), ((), ()))
OFFSETS = list(itertools.product((-1, 0, 1), repeat=3))
POS_HI, POS_MID, POS_LO, POS_OFF, LABEL = 64, 72, 80, 88, 96
GATHERED = 96


def dot(a, b):
    return jnp.dot(a, b, preferred_element_type=f32)


def dot_nt(a, b):
    return lax.dot_general(a, b, NT, preferred_element_type=f32)


def split2(x):
    hi = x.astype(bf16)
    return hi, (x - hi.astype(f32)).astype(bf16)


def sincos_turns(u):
    q = jnp.round(u * 2.0)
    x = (u - 0.5 * q) * (2.0 * math.pi)
    odd = q - 2.0 * jnp.floor(q * 0.5)
    sign = 1.0 - 2.0 * odd
    y = x * x
    s = -1.0 / 39916800.0
    for c in (1.0 / 362880.0, -1.0 / 5040.0, 1.0 / 120.0, -1.0 / 6.0, 1.0):
        s = s * y + c
    c_ = 1.0 / 479001600.0
    for c in (-1.0 / 3628800.0, 1.0 / 40320.0, -1.0 / 720.0, 1.0 / 24.0, -0.5, 1.0):
        c_ = c_ * y + c
    return c_ * sign, s * x * sign


def phase_kernel(h_ref, dy_ref, geo_ref, mil_ref,
                 cos_ref, sin_ref, part_ref, table_ref, extra_ref):
    channels, atoms = h_ref.shape
    rows = mil_ref.shape[0]
    step = 128
    h = h_ref[...]
    stacked = jnp.concatenate([h, dy_ref[...]], axis=0)
    pos = geo_ref[0:8, :]
    hi = pos.astype(bf16).astype(f32)
    mid = (pos - hi).astype(bf16).astype(f32)
    lo = pos - hi - mid
    blank = jnp.zeros((LANES - LABEL - 8, atoms), f32)
    feats = jnp.concatenate(
        [h.astype(f32), hi, mid, lo, jnp.zeros((8, atoms), f32), geo_ref[16:24, :], blank], axis=0)
    table = jnp.transpose(feats).astype(bf16)
    inner = 27 * 16
    table_ref[...] = table[:inner].reshape(table_ref.shape)
    extra_ref[...] = table[inner:].reshape(extra_ref.shape)
    w0, w1, w2 = geo_ref[8:9, :], geo_ref[9:10, :], geo_ref[10:11, :]

    def body(i, _):
        at = pl.ds(pl.multiple_of(i * step, step), step)
        m = mil_ref[at, :]
        u = m[:, 0:1] * w0 + m[:, 1:2] * w1 + m[:, 2:3] * w2
        c, s = sincos_turns(u)
        c = c.astype(bf16)
        s = s.astype(bf16)
        cos_ref[at, :] = c
        sin_ref[at, :] = s
        part_ref[at, 0:2 * channels] = dot_nt(c, stacked).astype(bf16)
        part_ref[at, 2 * channels:4 * channels] = dot_nt(s, stacked).astype(bf16)
        return 0

    lax.fori_loop(0, rows // step, body, 0)


def coords(linear, sizes):
    nx, ny, nz = sizes
    return (linear // (ny * nz), (linear // nz) % ny, linear % nz)


def my_linear(sizes):
    nx, ny, nz = sizes
    return (lax.axis_index("gx") * ny + lax.axis_index("gy")) * nz + lax.axis_index("gz")


def neighbour(offset, sizes, sign):
    return tuple(lax.rem(lax.axis_index(a) + (n + sign * o), n)
                 for a, o, n in zip(AXES, offset, sizes))


def enter(n, sizes):
    me = my_linear(sizes)
    barrier = pltpu.get_barrier_semaphore()

    def signal(i, _):
        pl.semaphore_signal(barrier, inc=1, device_id=coords(lax.rem(me + i, n), sizes),
                            device_id_type=pl.DeviceIdType.MESH)
        return 0

    lax.fori_loop(1, n, signal, 0)
    pl.semaphore_wait(barrier, n - 1)
    return me


def span(o):
    return pl.ds(1, 3) if o == 0 else pl.ds(4 if o > 0 else 0, 1)


def own_span(o):
    return pl.ds(0, 3) if o == 0 else pl.ds(0 if o > 0 else 2, 1)


def remote(src, dst, send, recv, to):
    return pltpu.make_async_remote_copy(
        src_ref=src, dst_ref=dst, send_sem=send, recv_sem=recv, device_id=to,
        device_id_type=pl.DeviceIdType.MESH)


def all_bytes(ref, count, sem):
    part = ref.at[pl.ds(0, count)]
    return pltpu.make_async_copy(part, part, sem)


def stage_orders(sizes):
    bits = [[(i, k) for k in range(n.bit_length() - 1)] for i, n in enumerate(sizes)]
    first = bits[0] + bits[1] + bits[2]
    second = bits[0][:1] + bits[2] + bits[0][1:] + bits[1]
    return first, second


def to_stream(x, sizes):
    n = sizes[0] * sizes[1] * sizes[2]
    lead, total = x.shape[:-1], x.shape[-1]
    half = total // n // 2
    names = [(i, k) for i, m in enumerate(sizes) for k in reversed(range(m.bit_length() - 1))]
    y = x.reshape(lead + (2,) * len(names) + (2, half))
    parts = []
    for t, order in enumerate(stage_orders(sizes)):
        z = y[..., t, :]
        axes = (list(range(len(lead))) + [len(lead) + names.index(q) for q in order]
                + [z.ndim - 1])
        parts.append(jnp.transpose(z, axes).reshape(lead + (n * half,)))
    return jnp.concatenate(parts, axis=-1)


def short_kernel(sizes, basis_count, norm_atoms, norm_k,
                 table_ref, extra_ref, part_ref, kf_ref, nbr_ref, geo_ref, dy_ref, mix_ref,
                 gain_ref, shift_ref, dk_ref, dkt_ref,
                 home_ref, homex_ref, coefs_ref, fg_ref, weight_ref, radial_ref, own_ref,
                 halo, oh, near, filt, vals, ht, zg, acc, agg, gout, psum, rad,
                 grad, back, rb, sb, rf, sf, total, gbuf, wx, wy, wz, wout,
                 hs, hr, bs, br, rss, rsr, ags, agr, wss, wsr):
    n = sizes[0] * sizes[1] * sizes[2]
    ep = oh.shape[1]
    nbr, atoms = nbr_ref.shape
    channels = dy_ref.shape[0]
    orders = stage_orders(sizes)
    stages = len(orders[0])
    enter(n, sizes)
    mine = [lax.axis_index(a) for a in AXES]

    def slot_of(o):
        return 9 * (o[0] + 1) + 3 * (o[1] + 1) + o[2] + 1

    steps = [o for o in OFFSETS if o != (0, 0, 0)]
    halos = [remote(table_ref.at[tuple(own_span(d) for d in o)],
                    halo.at[tuple(span(d) for d in o)],
                    hs.at[slot_of(o)], hr.at[slot_of(o)], neighbour(o, sizes, -1))
             for o in steps]
    for copy in halos:
        copy.start()

    def bit_of(t, s):
        axis, k = orders[t][s]
        b = (mine[axis] // (2 ** k)) % 2
        to = tuple(m + (1 - 2 * b) * (2 ** k) if i == axis else m for i, m in enumerate(mine))
        return b, to

    lows = []
    for t in range(2):
        low = [0]
        for s in range(stages):
            low.append(low[-1] + bit_of(t, s)[0] * (n >> (s + 1)))
        lows.append(low)

    wide = [s for s in range(stages) if (n >> (s + 1)) <= 2]

    def place_of(s):
        if s in wide:
            return sum(n >> (q + 1) for q in wide if q < s)
        return sum(n >> (q + 1) for q in range(s))

    def scatter_copy(t, s):
        half = n >> (s + 1)
        b, to = bit_of(t, s)
        at = pl.ds(place_of(s), half)
        if s in wide:
            src, dst = sf.at[t, at], rf.at[t, at]
        else:
            src = part_ref.at[t, pl.ds((1 - b) * half, half)] if s == 0 else sb.at[t, at]
            dst = rb.at[t, at]
        return remote(src, dst, rss.at[t * stages + s], rsr.at[t * stages + s], to)

    def scatter_start(s):
        half = n >> (s + 1)
        for t in range(2):
            b, _ = bit_of(t, s)
            if s > 0:
                out = sf if s in wide else sb

                def fill(i, _, t=t, b=b, out=out):
                    out[t, place_of(s) + i] = total[t, (1 - b) * half + i].astype(out.dtype)
                    return 0

                lax.fori_loop(0, half, fill, 0)
            scatter_copy(t, s).start()

    def scatter_end(s):
        half = n >> (s + 1)
        for t in range(2):
            b, _ = bit_of(t, s)
            scatter_copy(t, s).wait()
            got = rf if s in wide else rb
            old = part_ref if s == 0 else total

            def fold(i, _, t=t, b=b, got=got, old=old):
                total[t, i] = (old[t, b * half + i].astype(f32)
                               + got[t, place_of(s) + i].astype(f32))
                return 0

            lax.fori_loop(0, half, fold, 0)

    def gather_copy(t, s):
        held = n >> (s + 1)
        _, to = bit_of(t, s)
        part = gbuf.at[t, pl.ds(lows[t][s + 1], held)]
        return remote(part, part, ags.at[t * stages + s], agr.at[t * stages + s], to)

    scatter_start(0)
    for copy in halos:
        copy.wait()
    halo[1:4, 1:4, 1:4] = table_ref[...]
    cells = 125 * 16
    extras = extra_ref.shape[0] * 16
    pad = ep - cells - extras
    table = jnp.concatenate(
        [halo[...].reshape(cells, LANES), extra_ref[...].reshape(extras, LANES),
         jnp.zeros((pad, LANES), bf16)], axis=0)
    tf = table.astype(f32)
    label = tf[:, LABEL:LABEL + 1]
    gtable = jnp.concatenate(
        [gain_ref[...], jnp.ones((gain_ref.shape[0], LANES - channels), f32)], axis=1)
    gains = jnp.zeros((ep, LANES), f32)
    for s in range(gain_ref.shape[0]):
        gains = jnp.where(label == float(s), gtable[s:s + 1, :], gains)
    zg[...] = gains
    mix = jnp.concatenate(
        [jnp.concatenate([mix_ref[...], jnp.zeros((channels, LANES - channels), bf16)], axis=1),
         jnp.zeros((LANES - channels, LANES), bf16)], axis=0)
    z = dot(table, mix) * gains
    lane = lax.broadcasted_iota(jnp.int32, (ep, LANES), 1)
    full = jnp.where(lane < channels, z, tf) + shift_ref[...]
    vals[...] = jnp.transpose(full).astype(bf16)
    ht[...] = jnp.transpose(tf).astype(bf16)
    spacing = reach_sq / (basis_count - 1)
    centre = lax.broadcasted_iota(jnp.int32, (basis_count, 1), 0).astype(f32) * spacing
    inv = 1.0 / (2.0 * spacing)
    own = geo_ref[0:8, :]
    agg[...] = jnp.zeros_like(agg)
    psum[...] = jnp.zeros_like(psum)
    acc[...] = jnp.zeros_like(acc)
    rad[...] = jnp.zeros_like(rad)
    one, nil = jnp.ones((), bf16), jnp.zeros((), bf16)
    dkt_hi, dkt_lo = split2(dkt_ref[...])
    dkt3 = jnp.concatenate([dkt_hi, dkt_lo, dkt_hi], axis=1)
    dk_hi, dk_lo = split2(dk_ref[...])
    dk3 = jnp.concatenate([dk_hi, dk_lo, dk_hi], axis=1)
    tile = 256

    def thirds(v):
        a = (v >= 9).astype(jnp.int32) + (v >= 18).astype(jnp.int32)
        r = v - 9 * a
        b = (r >= 3).astype(jnp.int32) + (r >= 6).astype(jnp.int32)
        return a, b, r - 3 * b

    def compact(e):
        slot = e // atoms
        atom = e - slot * atoms
        block = atom // 16
        o = thirds(slot)
        t = thirds(jnp.minimum(block, 26))
        x, y, w = [ti - 1 + 3 * (oi - 1) + 2 for ti, oi in zip(t, o)]
        cell = jnp.where(block < 27, 25 * x + 5 * y + w, 125 - 27 + block)
        return cell * 16 + (atom - block * 16)

    def geometry(j):
        at = near[j]
        place = at[POS_HI:POS_HI + 8] + at[POS_MID:POS_MID + 8] + at[POS_LO:POS_LO + 8]
        rel = (place + at[POS_OFF:POS_OFF + 8]) - own
        d2 = jnp.sum(rel * rel, axis=0, keepdims=True)
        arg = (d2 - centre) * inv
        return at, rel, arg, jnp.exp(-(arg * arg))

    def forward(j, _):
        cid = compact(nbr_ref[pl.ds(j, 1), :])
        high = cid // tile
        low = cid - high * tile
        for start in range(0, ep, tile):
            size = min(tile, ep - start)
            want = jnp.where(high == start // tile, low, -1).astype(f32).astype(bf16)
            rows = lax.broadcasted_iota(jnp.int32, (size, atoms), 0).astype(f32).astype(bf16)
            oh[j, start:start + size, :] = jnp.where(rows == want, one, nil)
        near[j] = dot(vals[0:GATHERED, :], oh[j])
        at, rel, arg, basis = geometry(j)
        b_hi, b_lo = split2(basis)
        f = dot(dkt3, jnp.concatenate([b_hi, b_hi, b_lo], axis=0))
        filt[j] = f
        agg[...] += f * at[0:channels]
        return 0

    cuts = [nbr * i // stages for i in range(stages + 1)]
    for s in range(stages):
        lax.fori_loop(cuts[s], cuts[s + 1], forward, 0)
        scatter_end(s)
        if s + 1 < stages:
            scatter_start(s + 1)
    ch = channels
    for t in range(2):
        rows = total[t, 0]
        hc = rows.shape[0]
        kf = kf_ref[t]
        cst = rows[:, 0:ch] * norm_atoms
        cbk = rows[:, ch:2 * ch] * norm_k
        sst = rows[:, 2 * ch:3 * ch] * norm_atoms
        sbk = rows[:, 3 * ch:4 * ch] * norm_k
        gbuf[t, lows[t][stages]] = jnp.concatenate(
            [norm_atoms * kf * cbk, norm_k * kf * cst, norm_atoms * kf * sbk,
             norm_k * kf * sst], axis=1).astype(bf16)
        fg_ref[t] = cst * cbk + sst * sbk
    for t in range(2):
        gather_copy(t, stages - 1).start()
    scale = nbr ** (-0.5)
    v = agg[...] * scale
    sg = 1.0 / (1.0 + jnp.exp(-v))
    gout[...] = dy_ref[...].astype(f32) * (sg * (1.0 + v * (1.0 - sg))) * scale

    def backward(j, _):
        g = gout[...]
        at, rel, arg, basis = geometry(j)
        dz = (filt[j] * g).astype(bf16)
        df_hi, df_lo = split2(at[0:channels] * g)
        db = dot(dk3, jnp.concatenate([df_hi, df_hi, df_lo], axis=0))
        dd2 = jnp.sum(db * basis * arg, axis=0, keepdims=True) * (-2.0 * inv)
        drel = 2.0 * rel * dd2
        psum[...] += drel
        d_hi = drel.astype(bf16).astype(f32)
        dvals = jnp.concatenate(
            [dz, jnp.concatenate([d_hi, drel - d_hi], axis=0).astype(bf16)], axis=0)
        acc[...] += dot_nt(oh[j], dvals)
        b_hi, b_lo = split2(basis)
        rad[...] += dot_nt(jnp.concatenate([b_hi, b_lo, b_hi], axis=1),
                           jnp.concatenate([df_hi, df_hi, df_lo], axis=1))
        return 0

    for i in range(stages):
        lax.fori_loop(cuts[i], cuts[i + 1], backward, 0)
        s = stages - 1 - i
        for t in range(2):
            gather_copy(t, s).wait()
            if s > 0:
                gather_copy(t, s - 1).start()
    g = acc[...]
    zgrad = g[:, 0:channels]
    pg = g[:, channels:channels + 8] + g[:, channels + 8:channels + 16]
    p_hi = pg.astype(bf16).astype(f32)
    rows = jnp.concatenate(
        [zgrad, p_hi, pg - p_hi, jnp.zeros((ep, LANES - channels - 16), f32)], axis=1)
    scaled = rows * zg[...]
    grad[...] = rows[0:cells].astype(bf16).reshape(grad.shape)
    returns = []
    for o in steps:
        loc = (slot_of(o),) + tuple(pl.ds(0, 3 if d == 0 else 1) for d in o)
        copy = remote(grad.at[tuple(span(d) for d in o)], back.at[loc],
                      bs.at[slot_of(o)], br.at[slot_of(o)], neighbour(o, sizes, 1))
        copy.start()
        returns.append(copy)
    homex_ref[...] = scaled[cells:cells + extras]
    own_ref[...] = psum[...]
    w = dot(ht[0:channels, :], scaled[:, 0:channels].astype(bf16))
    half = channels // 2
    r = rad[...]
    hb = basis_count // 2
    small = jnp.concatenate(
        [jnp.concatenate([w[:half], w[half:]], axis=1),
         jnp.concatenate([r[:hb], r[hb:]], axis=1)], axis=0)

    def small_start(axis, buf, value):
        count = sizes[axis]
        at = mine[axis]
        wout[axis] = value
        for i in range(1, count):
            to = tuple(lax.rem(m + i, count) if k == axis else m for k, m in enumerate(mine))
            remote(wout.at[axis], buf.at[at], wss.at[axis], wsr.at[axis], to).start()

    def small_end(axis, buf):
        count = sizes[axis]
        all_bytes(buf, count - 1, wss.at[axis]).wait()
        all_bytes(buf, count - 1, wsr.at[axis]).wait()
        buf[mine[axis]] = wout[axis]
        return jnp.sum(buf[...], axis=0)

    def land(group):
        for o, copy in group:
            copy.wait()
            at = tuple(slice(0, 3) if d == 0 else (slice(0, 1) if d > 0 else slice(2, 3))
                       for d in o)
            loc = (slot_of(o),) + tuple(slice(0, 3 if d == 0 else 1) for d in o)
            home_ref[at] += back[loc].astype(f32)

    pairs = sorted(zip(steps, returns), key=lambda p: sum(abs(d) for d in p[0]))
    small_start(0, wx, small)
    coefs_ref[...] = gbuf[...]
    home_ref[...] = rows[0:cells].reshape(grad.shape)[1:4, 1:4, 1:4]
    small = small_end(0, wx)
    small_start(1, wy, small)
    land(pairs[:6])
    small = small_end(1, wy)
    small_start(2, wz, small)
    land(pairs[6:])
    home_ref[...] *= zg[0:cells, :].reshape(5, 5, 5, 16, LANES)[1:4, 1:4, 1:4]
    small = small_end(2, wz)
    weight_ref[0:half] = small[0:half, 0:channels]
    weight_ref[half:channels] = small[0:half, channels:2 * channels]
    radial_ref[0:hb] = small[half:half + hb, 0:channels]
    radial_ref[hb:basis_count] = small[half:half + hb, channels:2 * channels]


def final_kernel(sizes, coef_ref, cos_ref, sin_ref, h_ref, dy_ref, milt_ref, home_ref,
                 extra_ref, own_ref, mix_ref, atom_ref, pos_ref, eh, ep_):
    rows = coef_ref.shape[0]
    channels, atoms = h_ref.shape
    step = 256
    stacked = jnp.concatenate([h_ref[...], dy_ref[...]], axis=0)
    eh[...] = jnp.zeros_like(eh)
    ep_[...] = jnp.zeros_like(ep_)

    def body(i, _):
        at = pl.ds(pl.multiple_of(i * step, step), step)
        piece = coef_ref[at, :]
        c, s = cos_ref[at, :], sin_ref[at, :]
        turned = jnp.transpose(piece.astype(f32)).astype(bf16)
        eh[...] += dot(turned[0:channels], c) + dot(turned[2 * channels:3 * channels], s)
        u = dot(piece[:, 0:2 * channels], stacked)
        v = dot(piece[:, 2 * channels:4 * channels], stacked)
        hi, lo = split2(v * c.astype(f32) - u * s.astype(f32))
        m = milt_ref[i]
        ep_[...] += dot(m, hi) + dot(m, lo)
        return 0

    lax.fori_loop(0, rows // step, body, 0)
    blocks = 27 * 16
    home = jnp.concatenate(
        [home_ref[...].reshape(blocks, LANES),
         extra_ref[...]], axis=0)
    g = jnp.transpose(home)
    zscaled = g[0:channels].astype(bf16)
    short = dot(mix_ref[...], zscaled)
    atom_ref[...] = (dy_ref[...].astype(f32) + eh[...] + short).astype(bf16)
    pos_short = g[channels:channels + 8] + g[channels + 8:channels + 16] - own_ref[...]
    pos_short = pos_short[0:3]
    for d in range(3):
        pos_ref[d:d + 1] = ep_[d:d + 1] * (2.0 * math.pi / sizes[d]) + pos_short[d:d + 1]


def vmem(count):
    return [pl.BlockSpec(memory_space=pltpu.VMEM)] * count


def params(**more):
    return pltpu.CompilerParams(vmem_limit_bytes=VMEM_LIMIT, **more)


def shards(sizes, atom_embedding, output_adjoint, fractional_coords, element_labels,
           adjacent_ghost_entries, miller_triples, reciprocal_kernel, channel_mixing_matrix,
           element_channel_factor, distance_kernel):
    n = sizes[0] * sizes[1] * sizes[2]
    shape = jax.ShapeDtypeStruct
    h = atom_embedding[0, 0, 0]
    dy = output_adjoint[0, 0, 0]
    pos = fractional_coords[0, 0, 0]
    channels, atoms = h.shape
    rows = miller_triples.shape[1]
    share = rows // n
    hs = share // 2
    basis_count = distance_kernel.shape[0]
    norm_atoms = (atoms * n) ** (-0.5)
    norm_k = rows ** (-0.5)
    counts = jnp.array(sizes, f32)
    anchor = jnp.stack([lax.axis_index(a) for a in AXES]).astype(f32)
    gap = jnp.zeros((5, atoms), f32)
    geo = jnp.concatenate(
        [pos, gap, (pos + anchor[:, None]) / counts[:, None], gap,
         element_labels[0, 0].astype(f32), jnp.zeros((7, atoms), f32)], axis=0)
    miller = to_stream(miller_triples.astype(f32), sizes)
    mil8 = jnp.pad(miller.T, ((0, 0), (0, 5)))
    extras = atoms // 16 - 27
    cos_all, sin_all, part, table, extra = pl.pallas_call(
        phase_kernel,
        out_shape=(shape((rows, atoms), bf16), shape((rows, atoms), bf16),
                   shape((rows, 4 * channels), bf16), shape((3, 3, 3, 16, LANES), bf16),
                   shape((extras, 16, LANES), bf16)),
        in_specs=vmem(4), out_specs=tuple(vmem(5)), compiler_params=params(), name="phases",
    )(h, dy, geo, mil8)

    me = lax.axis_index(AXES)
    kf = lax.dynamic_slice_in_dim(reciprocal_kernel, me * share, share, 0)
    dma = pltpu.SemaphoreType.DMA
    nbr = adjacent_ghost_entries.shape[3]
    ep = -(-((125 + extras) * 16) // LANES) * LANES
    shift = np.zeros((ep, LANES), np.float32)
    for i, cell in enumerate(itertools.product(range(5), repeat=3)):
        for d, q in enumerate(cell):
            shift[16 * i:16 * i + 16, POS_OFF + d] = -1.0 if q == 0 else (1.0 if q == 4 else 0.0)
    wr = channels // 2 + basis_count // 2
    stages = n.bit_length() - 1
    scratch = pltpu.VMEM
    home, homex, coefs, filter_share, weight_grad, radial_grad, own = pl.pallas_call(
        functools.partial(short_kernel, sizes, basis_count, norm_atoms, norm_k),
        out_shape=(shape((3, 3, 3, 16, LANES), f32), shape((extras * 16, LANES), f32),
                   shape((2, n, hs, 4 * channels), bf16), shape((2, hs, channels), f32),
                   shape((channels, channels), f32), shape((basis_count, channels), f32),
                   shape((8, atoms), f32)),
        in_specs=vmem(12), out_specs=tuple(vmem(7)),
        scratch_shapes=[scratch((5, 5, 5, 16, LANES), bf16),
                        scratch((nbr, ep, atoms), bf16),
                        scratch((nbr, GATHERED, atoms), f32),
                        scratch((nbr, channels, atoms), f32),
                        scratch((LANES, ep), bf16), scratch((LANES, ep), bf16),
                        scratch((ep, LANES), f32),
                        scratch((ep, channels + 16), f32),
                        scratch((channels, atoms), f32), scratch((channels, atoms), f32),
                        scratch((8, atoms), f32), scratch((basis_count, channels), f32),
                        scratch((5, 5, 5, 16, LANES), bf16),
                        scratch((27, 3, 3, 3, 16, LANES), bf16),
                        scratch((2, n, hs, 4 * channels), bf16),
                        scratch((2, n, hs, 4 * channels), bf16),
                        scratch((2, 4, hs, 4 * channels), f32),
                        scratch((2, 4, hs, 4 * channels), f32),
                        scratch((2, n // 2, hs, 4 * channels), f32),
                        scratch((2, n, hs, 4 * channels), bf16),
                        scratch((sizes[0], wr, LANES), f32),
                        scratch((sizes[1], wr, LANES), f32),
                        scratch((sizes[2], wr, LANES), f32),
                        scratch((3, wr, LANES), f32),
                        dma((27,)), dma((27,)), dma((27,)), dma((27,)),
                        dma((2 * stages,)), dma((2 * stages,)),
                        dma((2 * stages,)), dma((2 * stages,)), dma((3,)), dma((3,))],
        compiler_params=params(collective_id=0, has_side_effects=True), name="short",
    )(table, extra, part.reshape(2, n, hs, 4 * channels), kf.reshape(2, hs, channels),
      adjacent_ghost_entries[0, 0, 0], geo, dy, channel_mixing_matrix, element_channel_factor,
      jnp.asarray(shift), distance_kernel, distance_kernel.T)

    milt = jnp.pad(miller.astype(bf16), ((0, 13), (0, 0)))
    milt = jnp.transpose(milt.reshape(16, rows // 256, 256), (1, 0, 2))
    atom_grad, pos_grad = pl.pallas_call(
        functools.partial(final_kernel, sizes),
        out_shape=(shape((channels, atoms), bf16), shape((3, atoms), f32)),
        in_specs=vmem(10), out_specs=tuple(vmem(2)),
        scratch_shapes=[scratch((channels, atoms), f32), scratch((16, atoms), f32)],
        compiler_params=params(), name="final",
    )(coefs.reshape(rows, 4 * channels), cos_all, sin_all, h, dy, milt, home, homex, own,
      channel_mixing_matrix)
    return (atom_grad[None, None, None], pos_grad[None, None, None], weight_grad,
            radial_grad, filter_share.reshape(share, channels))


def solution(mesh):
    sizes = tuple(mesh.shape[a] for a in AXES)
    brick = P("gx", "gy", "gz", None, None)
    return jax.shard_map(
        functools.partial(shards, sizes),
        mesh=mesh,
        in_specs=(brick, brick, brick, P("gx", "gy", "gz", None), brick,
                  P(), P(), P(), P(), P()),
        out_specs=(brick, brick, P(), P(), P(("gx", "gy", "gz"), None)),
        check_vma=False,
    )
```

time: 155 us -> 105 us (0.68)
  Pallas kernels: 133 us -> 90.7 us
  local copies, waits for them, and re-layouts: 17.6 us -> 10.8 us
    pallas_call x4 -> x2, Pallas kernels: 120 us -> 77.8 us  [the longest x1 69.3 us: shards(): pl.pallas_call(functools.partial(short_kernel, sizes, basis_count, norm_a...]
    slice x4 -> x1, local copies, waits for them, and re-layouts: 6.12 us -> 0.08 us  [to_stream(): z = y[..., t, :]]
    pad x5 -> x0, local copies, waits for them, and re-layouts: 3.03 us -> none  [the longest x1 0.62 us: shards(): jnp.pad(channel_mixing_matrix, ((0, LANES - channels), (0, LANES - channe...]
    concatenate x0 -> x3, local copies, waits for them, and re-layouts: none -> 2.23 us  [the longest x1 1.86 us: shards(): jnp.concatenate([pos, gap, (pos + anchor[:, None]) / counts[:, None], gap...]
    unnamed x29 -> x19, local copies, waits for them, and re-layouts: 4.89 us -> 5.62 us
where the time goes in v1:
time: 105 us
  Pallas kernels  90.7 us (86%)
  local copies, waits for them, and re-layouts  10.8 us (10%)
  other arithmetic  2.31 us (2%)
    pallas_call x1, Pallas kernels, shards(): pl.pallas_call(functools.partial(short_kernel, sizes, basis_count, norm_a...  69.3 us
    pallas_call x1, Pallas kernels, shards(): pl.pallas_call(phase_kernel, out_shape=(shape((rows, atoms), bf16), shape...  12.9 us
    pallas_call x1, Pallas kernels, shards(): pl.pallas_call(functools.partial(final_kernel, sizes), out_shape=(shape((...  8.53 us
    unnamed x19, local copies, waits for them, and re-layouts  5.62 us

profile of v1, /device:TPU:0, one launch (start us, length us, event | category | flops | bytes accessed | tf_op | source)
XLA Modules:
  0.0 104.5 jit_solution(6799341114306409897)
XLA Ops:
  0.6 0.0 copy-start
  0.7 1.0 copy-done
  1.7 0.1 constant_dynamic-slice_fusion
  1.8 0.7 copy.32
  2.5 0.1 add_convert_fusion
  2.5 0.8 add_multiply_fusion
  3.3 0.7 copy.49
  4.0 0.7 convert_bitcast_fusion
  4.7 1.9 %concatenate.10.geo_ref = f32[24,512]{1,0:T(8,128)} concatenate(f32[3,512]{1,0:T(4,128)S(1)} %bitcast.53, f32[5,512]{1,0:T(8,128)S(1)} %broadcast_in_dim.14, f32[3,512]{1,0:T(4,128)S(1)} %add_multiply_fusion, f32[5,512]{1,0:T(8,128)S(1)} %broadcast_in_dim.14, f32[1,512]{1,0:T(1,128)S(1)} %convert_bitcast_fusion, f32[7,512]{1,0:T(8,128)S(1)} %broadcast_in_dim.15), dimensions={0} | concatenate | bytes 98304 | tf_op jit(solution)/shard_map/concatenate | solution.py:514
  6.6 0.8 convert_element_type.34
  7.3 0.1 reshape.73
  7.5 0.1 fusion
  7.6 0.1 reshape.74
  7.7 0.1 reshape.75
  7.9 0.0 copy-start.1
  7.9 0.4 copy.31
  8.2 1.1 %pad.8.mil_ref = f32[2048,8]{1,0:T(8,128)} pad(f32[2048,3]{1,0:T(8,128)S(1)} %bitcast.38, f32[]{:T(128)} %constant.12.clone.1), padding=0_0x0_5 | pad | bytes 90116 | tf_op jit(solution)/shard_map/jit(_pad)/pad | solution.py:518
  9.3 12.9 %phases.1 = (bf16[2048,512]{1,0:T(8,128)(2,1)}, bf16[2048,512]{1,0:T(8,128)(2,1)}, bf16[2048,256]{1,0:T(8,128)(2,1)}, bf16[3,3,3,16,128]{4,3,2,1,0:T(8,128)(2,1)}, bf16[5,16,128]{2,1,0:T(8,128)(2,1)}) custom-call(bf16[64,512]{1,0:T(8,128)(2,1)} %bitcast.44, bf16[64,512]{1,0:T(8,128)(2,1)} %bitcast.41, f32[24,512]{1,0:T(8,128)} %concatenate.10.geo_ref, ...), custom_call_target="tpu_custom_call" | custom-call | tf_op jit(solution)/shard_map/phases/pallas_call | solution.py:520
  22.2 0.0 copy-done.1
  22.2 0.7 copy.33
  22.9 69.3 %short.1 = (f32[3,3,3,16,128]{4,3,2,1,0:T(8,128)}, f32[80,128]{1,0:T(8,128)}, bf16[2,32,32,256]{3,2,1,0:T(8,128)(2,1)}, f32[2,32,64]{2,1,0:T(8,128)}, f32[64,64]...) custom-call(bf16[3,3,3,16,128]{4,3,2,1,0:T(8,128)(2,1)} %get-tuple-element.19.table_ref, ...), custom_call_target="tpu_custom_call" | custom-call | tf_op jit(solution)/shard_map/short/pallas_call | solution.py:540
  92.3 0.6 copy.46
  92.9 0.0 copy-start.3
  92.9 0.0 copy-start.4
  92.9 8.5 %final.1 = (bf16[64,512]{1,0:T(8,128)(2,1)}, f32[3,512]{1,0:T(4,128)}) custom-call(bf16[2048,256]{1,0:T(8,128)(2,1)} %bitcast.40, bf16[2048,512]{1,0:T(8,128)(2,1)} %get-tuple-element.23.cos_ref, bf16[2048,512]{1,0:T(8,128)(2,1)} %get-tuple-element.24.sin_ref, bf16[64,512]{1,0:T(8,128)(2,1)} %bitcast.45, bf16[64,512]{1,0:T(8,128)(2,1)} %bitcast.43, ...), custom_call_target="tpu_custom_call" | custom-call | tf_op jit(solution)/shard_map/final/pallas_call | solution.py:578
  101.4 1.3 %copy.35 = f32[1,1,1,3,512]{4,2,3,1,0:T(1,128)} copy(f32[1,1,1,3,512]{4,3,2,1,0:T(4,128)} %bitcast.55) | data formatting | bytes 12288
  102.7 0.0 copy-done.3
  102.7 0.6 copy.54
  103.3 0.0 copy-done.4
  103.3 0.6 copy.55
  103.9 0.0 copy-done.2
  103.9 0.6 copy.56
  (9 shorter events, 0.1 us)
Async XLA Ops:
  0.6 1.0 %copy-start = (f32[2048,64]{0,1:T(8,128)S(1)}, f32[2048,64]{0,1:T(8,128)}, u32[]{:S(2)}) copy-start(f32[2048,64]{0,1:T(8,128)} %param.18) | copy-start | bytes 1572868
  7.9 14.4 %copy-start.1 = (f32[16,64]{1,0:T(8,128)S(1)}, f32[16,64]{1,0:T(8,128)}, u32[]{:S(2)}) copy-start(f32[16,64]{1,0:T(8,128)} %dk_ref.1) | copy-start | bytes 12292
  92.9 9.8 %copy-start.3 = (f32[64,64]{1,0:T(8,128)S(1)}, f32[64,64]{1,0:T(8,128)}, u32[]{:S(2)}) copy-start(f32[64,64]{1,0:T(8,128)} %get-tuple-element.57) | copy-start | bytes 49156
  92.9 10.5 %copy-start.4 = (f32[16,64]{1,0:T(8,128)S(1)}, f32[16,64]{1,0:T(8,128)}, u32[]{:S(2)}) copy-start(f32[16,64]{1,0:T(8,128)} %get-tuple-element.58) | copy-start | bytes 12292
  92.9 11.1 %copy-start.2 = (f32[2,32,64]{2,1,0:T(8,128)S(1)}, f32[2,32,64]{2,1,0:T(8,128)}, u32[]{:S(2)}) copy-start(f32[2,32,64]{2,1,0:T(8,128)} %get-tuple-element.32) | copy-start | bytes 49156
